TPU v7x, 32 devices: a whole 2x2x4 slice. The times are simulated.
32 devices in a mesh: py: 8 (over y, x, core), pz: 4 (over z).
Axes of the slice: x: 2, y: 2, z: 4, core: 2. Of those that a mesh axis runs over, the one named last changes fastest.
Arguments:
- velocity: float32 [3, 320, 320, 320], P(None, 'py', 'pz'), may hold values from -12 to 12
Outputs:
- filtered_velocity: float32 [3, 128, 128, 128], P(None, 'py', 'pz')
- subgrid_stress: float32 [6, 128, 128, 128], P(None, 'py', 'pz')
All inputs are finite; a program needn't handle non-finite values.
Results may differ from a plain program's by a relative error of at most 0.000082.
Values sent between devices are 32-bit elements; how exact they have to be, the bound alone decides.
A program may use at most 128 MiB of HBM per device.

v0:
```python
import functools
import math

import jax
import jax.numpy as jnp
import ml_dtypes
import numpy as np
from jax import lax
from jax.experimental import pallas as pl
from jax.experimental.pallas import tpu as pltpu
from jax.sharding import PartitionSpec as P

M = 128

factor_pairs = ((0, 0), (0, 1), (0, 2), (1, 1), (1, 2), (2, 2))
fields_count = 9
LANES = 128


def line_filter(fine, coarse):
    half = coarse // 2
    modes = np.arange(1, half)
    width = 2.0 * math.pi / coarse
    gain = np.exp(-(modes.astype(np.float64) ** 2) * (width * width / 24.0))
    turns = np.arange(coarse)[:, None] * fine - np.arange(fine)[None, :] * coarse
    period = fine * coarse
    matrix = np.ones((coarse, fine))
    for mode, weight in zip(modes, gain):
        matrix += 2.0 * weight * np.cos(2.0 * math.pi * ((mode * turns) % period) / period)
    return (matrix / fine).astype(np.float32)


def halves(matrix):
    top = matrix.astype(ml_dtypes.bfloat16)
    return top, (matrix - top.astype(np.float32)).astype(ml_dtypes.bfloat16)


def split(value):
    top = value.astype(jnp.bfloat16)
    return top, (value - top.astype(jnp.float32)).astype(jnp.bfloat16)


def dot(left, right):
    return jnp.dot(left, right, preferred_element_type=jnp.float32)


def rows_times(value, table):
    width = table.shape[1] // 2
    top, rest = split(value)
    both = dot(top, table)
    return both[:, :width] + both[:, width:] + dot(rest, table[:, :width])


def kernel(
    rows, columns, velocity, third, second, first, filtered, stress,
    fine, lines, send_z, recv_z, send_y, recv_y, turned,
    load_sem, send_z_sem, recv_z_sem, send_y_sem, recv_y_sem,
):
    me_y = lax.axis_index("py")
    me_z = lax.axis_index("pz")
    steps = fine.shape[1]
    depth = fine.shape[3]
    block = LANES // columns
    band = filtered.shape[1]
    MESH = pl.DeviceIdType.MESH

    def load(c):
        return pltpu.make_async_copy(velocity.at[c], fine.at[c], load_sem.at[c])

    for c in range(3):
        load(c).start()

    barrier = pltpu.get_barrier_semaphore()
    for k in range(1, columns):
        pl.semaphore_signal(
            barrier, inc=1, device_id=(me_y, (me_z + k) % columns), device_id_type=MESH
        )
    for j in range(1, rows):
        pl.semaphore_signal(
            barrier, inc=1, device_id=((me_y + j) % rows, me_z), device_id_type=MESH
        )
    pl.semaphore_wait(barrier, columns + rows - 2)

    def copy_z(f, k, at=0, count=2):
        return pltpu.make_async_remote_copy(
            src_ref=send_z.at[f, k - 1, pl.ds(2 * at, count)],
            dst_ref=recv_z.at[f, k, pl.ds(2 * at, count)],
            send_sem=send_z_sem.at[f, k - 1],
            recv_sem=recv_z_sem.at[f, k - 1, at],
            device_id=(me_y, (me_z + k) % columns),
            device_id_type=MESH,
        )

    def copy_y(f, j, at=0, count=2):
        return pltpu.make_async_remote_copy(
            src_ref=send_y.at[f, j - 1, pl.ds(2 * at, count)],
            dst_ref=recv_y.at[f, pl.ds(j * steps + 2 * at, count)],
            send_sem=send_y_sem.at[f, j - 1],
            recv_sem=recv_y_sem.at[f, j - 1],
            device_id=((me_y + rows - j) % rows, me_z),
            device_id_type=MESH,
        )

    def pair_of(f):
        return f // 6 + f // 8, f - 3 - 2 * (f // 6) - f // 8

    half = steps // 2

    def contract_third(f, product):
        if product:
            left, right = pair_of(f)
        else:
            left = right = f

        def piece(t, carry):
            u, b = t // columns, t % columns
            where = pl.ds(2 * u, 2)
            value = fine[left, where, b]
            if product:
                value = value * fine[right, where, b]
            value = value.reshape(2 * depth, value.shape[-1])
            lines[b] = rows_times(value, third[b]).reshape(2, depth, LANES)
            return carry

        def regroup(u, i):
            group = lax.broadcasted_iota(jnp.int32, (depth, LANES), 1) // block
            parts = [lines[b, i] for b in range(columns)]
            for k in range(columns):
                out = parts[-1]
                for b in range(columns - 1):
                    out = jnp.where(group == (me_z + k + b) % columns, parts[b], out)
                if k == 0:
                    recv_z[f, 0, 2 * u + i] = out
                else:
                    send_z[f, k - 1, 2 * u + i] = out

        def unit(u, carry):
            lax.fori_loop(u * columns, (u + 1) * columns, piece, 0)
            for i in range(2):
                regroup(u, i)
            for k in range(1, columns):
                copy_z(f, k, u).start()
            return carry

        lax.fori_loop(0, half, unit, 0)

    def contract_second(f):
        def piece(h, carry):
            for k in range(1, columns):
                copy_z(f, k, h).wait_recv()
            value = jnp.concatenate(
                [recv_z[f, :, 2 * h + i].reshape(columns * depth, LANES) for i in range(2)], axis=1
            )
            top, rest = split(value)
            table = second[...]
            both = dot(table, top)
            out = both[:M] + both[M:] + dot(table[:M], rest)
            for i in range(2):
                for j in range(rows):
                    part = out[j * band : (j + 1) * band, i * LANES : (i + 1) * LANES]
                    if j == 0:
                        recv_y[f, 2 * h + i] = part
                    else:
                        send_y[f, j - 1, 2 * h + i] = part
            for j in range(1, rows):
                copy_y(f, j, h).start()
            return carry

        lax.fori_loop(0, half, piece, 0)

    def contract_first(f, product):
        for j in range(1, rows):
            copy_y(f, j, 0, steps).wait_recv()
        pad = jnp.zeros((LANES - rows * steps, LANES), jnp.float32)
        for m in range(band):
            plane = jnp.concatenate([recv_y[f, :, m, :], pad], axis=0).T
            for g in range(columns):
                turned[m * block : (m + 1) * block, g * LANES : (g + 1) * LANES] = plane[
                    g * block : (g + 1) * block
                ]
        out = rows_times(turned[...], first[...]).reshape(band, block, M)
        if product:
            left, right = pair_of(f)
            stress[f - 3] = out - filtered[left] * filtered[right]
        else:
            filtered[f] = out

    def loop(start, stop, *work):
        def body(f, carry):
            for one in work:
                one(f)
            return carry

        lax.fori_loop(start, stop, body, 0)

    loop(0, 3, lambda f: load(f).wait(), lambda f: contract_third(f, False))
    loop(3, fields_count, lambda f: contract_third(f, True))
    loop(0, 2, contract_second)
    loop(2, 5, contract_second, lambda f: contract_first(f - 2, False))
    loop(5, fields_count, contract_second, lambda f: contract_first(f - 2, True))
    loop(fields_count - 2, fields_count, lambda f: contract_first(f, True))

    def finish(f):
        for k in range(1, columns):
            copy_z(f, k, 0, steps).wait_send()
        for j in range(1, rows):
            copy_y(f, j, 0, steps).wait_send()

    loop(0, fields_count, finish)


def tables(fine, rows, columns):
    matrix = line_filter(fine, M)
    block, band, depth = M // columns, M // rows, fine // columns
    steps = fine // rows // columns
    top, rest = halves(matrix)
    third, second, first = [], [], []
    for b in range(columns):
        order = np.concatenate(
            [np.arange(block) + ((g - b) % columns) * block for g in range(columns)]
        )
        third.append(np.concatenate([top.T[:, order], rest.T[:, order]], axis=1))
    lines = np.concatenate([np.arange(band) + (-r % rows) * band for r in range(2 * rows)])
    for z in range(columns):
        order = np.concatenate(
            [np.arange(depth) + ((z - k) % columns) * depth for k in range(columns)]
        )
        second.append(np.stack([half[lines][:, order] for half in (top, rest)]))
        groups = []
        for g in range(columns):
            points = np.concatenate(
                [
                    (r % rows) * steps * columns + np.arange(steps) * columns + (g - z) % columns
                    for r in range(2 * rows)
                ]
            )
            groups.append(np.concatenate([top.T[points], rest.T[points]], axis=1))
        first.append(np.stack(groups))
    return np.stack(third), np.stack(second), np.stack(first)


def kernel_shards(velocity):
    rows, columns = lax.axis_size("py"), lax.axis_size("pz")
    me_y, me_z = lax.axis_index("py"), lax.axis_index("pz")
    _, lines, depth, fine = velocity.shape
    steps = lines // columns
    block, band = M // columns, M // rows
    third, second, first = tables(fine, rows, columns)
    second = lax.dynamic_slice(
        jnp.asarray(second), (me_z, 0, (rows - me_y) % rows * band, 0), (1, 2, M, fine)
    ).reshape(2 * M, fine)
    first = lax.dynamic_slice(
        jnp.asarray(first), (me_z, 0, me_y * steps, 0), (1, columns, rows * steps, 2 * M)
    )[0]
    first = jnp.pad(first, ((0, 0), (0, LANES - rows * steps), (0, 0)))
    first = first.reshape(columns * LANES, 2 * M)
    velocity = velocity.reshape(3, steps, columns, depth, fine)
    vmem = pl.BlockSpec(memory_space=pltpu.VMEM)
    dma = pltpu.SemaphoreType.DMA
    f32 = jnp.float32
    return pl.pallas_call(
        functools.partial(kernel, rows, columns),
        out_shape=(
            jax.ShapeDtypeStruct((3, band, block, M), f32),
            jax.ShapeDtypeStruct((6, band, block, M), f32),
        ),
        in_specs=[pl.BlockSpec(memory_space=pl.ANY), vmem, vmem, vmem],
        out_specs=(vmem, vmem),
        scratch_shapes=[
            pltpu.VMEM((3, steps, columns, depth, fine), f32),
            pltpu.VMEM((columns, 2, depth, LANES), f32),
            pltpu.VMEM((fields_count, columns - 1, steps, depth, LANES), f32),
            pltpu.VMEM((fields_count, columns, steps, depth, LANES), f32),
            pltpu.VMEM((fields_count, rows - 1, steps, band, LANES), f32),
            pltpu.VMEM((fields_count, rows * steps, band, LANES), f32),
            pltpu.VMEM((band * block, columns * LANES), f32),
            dma((3,)),
            dma((fields_count, columns - 1)),
            dma((fields_count, columns - 1, steps // 2)),
            dma((fields_count, rows - 1)),
            dma((fields_count, rows - 1)),
        ],
        compiler_params=pltpu.CompilerParams(
            collective_id=0, has_side_effects=True, vmem_limit_bytes=67_000_000
        ),
    )(velocity, jnp.asarray(third), second, first)


def plain_shards(velocity):
    matrix = jnp.asarray(line_filter(velocity.shape[3], M))
    components = [velocity[component] for component in range(3)]
    fields = jnp.stack(components + [components[a] * components[b] for a, b in factor_pairs])
    high = lax.Precision.HIGHEST
    third = jnp.einsum("fabk,mk->fabm", fields, matrix, precision=high)
    third = lax.all_to_all(third, "pz", split_axis=3, concat_axis=2, tiled=True)
    second = jnp.einsum("fabm,nb->fanm", third, matrix, precision=high)
    second = lax.all_to_all(second, "py", split_axis=2, concat_axis=1, tiled=True)
    coarse = jnp.einsum("fanm,pa->fnmp", second, matrix, precision=high)
    stress = jnp.stack(
        [coarse[3 + p] - coarse[a] * coarse[b] for p, (a, b) in enumerate(factor_pairs)]
    )
    return coarse[:3], stress


def shards(velocity):
    rows, columns = lax.axis_size("py"), lax.axis_size("pz")
    _, lines, depth, fine = velocity.shape
    whole_tiles = (
        M == LANES
        and lines % (2 * columns) == 0
        and depth % 16 == 0
        and (M // rows) % 8 == 0
        and (M // columns) % 8 == 0
        and rows * (lines // columns) <= LANES
    )
    return kernel_shards(velocity) if whole_tiles else plain_shards(velocity)


def solution(mesh):
    placed = P(None, "py", "pz", None)
    return jax.shard_map(
        shards, mesh=mesh, in_specs=(placed,), out_specs=(placed, placed), check_vma=False
    )
```

profile of v0, /device:TPU:0, one launch (start us, length us, event | category | flops | bytes accessed | tf_op | source)
XLA Modules:
  0.0 341.6 jit_solution(9517278539518396513)
XLA Ops:
  0.6 1.0 dynamic-slice_bitcast_fusion
  1.6 0.7 pad.4
  2.4 1.6 constant_dynamic-slice_fusion
  4.0 334.3 %shard_map.59 = (f32[3,16,32,128]{3,2,1,0:T(8,128)}, f32[6,16,32,128]{3,2,1,0:T(8,128)}) custom-call(f32[3,10,4,80,320]{4,3,2,1,0:T(8,128)} %bitcast.5, bf16[4,320,256]{2,1,0:T(8,128)(2,1)} %constant.43.clone.third, bf16[256,320]{1,0:T(8,128)(2,1)} %bitcast.7, bf16[512,256]{1,0:T(8,128)(2,1)} %bitcast.6), custom_call_target="tpu_custom_call" | custom-call | tf_op jit(solution)/shard_map/pallas_call | solution.py:261
  338.3 0.0 copy-start
  338.3 2.2 copy.8
  340.5 0.0 copy-done
  340.5 1.1 copy.9
Async XLA Ops:
  338.3 2.2 copy-start
where the time goes:
time: 342 us
  Pallas kernels  334 us (98%)
  local copies, waits for them, and re-layouts  6.65 us (2%)
    pallas_call x1, Pallas kernels, kernel_shards(): pl.pallas_call(functools.partial(kernel, rows, columns), out_shape=(jax.S...  334 us

commit v1 on v0

v1 whole, which is shorter than its diff:
```python
import functools
import math

import jax
import jax.numpy as jnp
import ml_dtypes
import numpy as np
from jax import lax
from jax.experimental import pallas as pl
from jax.experimental.pallas import tpu as pltpu
from jax.sharding import PartitionSpec as P

M = 128

factor_pairs = ((0, 0), (0, 1), (0, 2), (1, 1), (1, 2), (2, 2))
fields_count = 9
LANES = 128


def line_filter(fine, coarse):
    half = coarse // 2
    modes = np.arange(1, half)
    width = 2.0 * math.pi / coarse
    gain = np.exp(-(modes.astype(np.float64) ** 2) * (width * width / 24.0))
    turns = np.arange(coarse)[:, None] * fine - np.arange(fine)[None, :] * coarse
    period = fine * coarse
    matrix = np.ones((coarse, fine))
    for mode, weight in zip(modes, gain):
        matrix += 2.0 * weight * np.cos(2.0 * math.pi * ((mode * turns) % period) / period)
    return (matrix / fine).astype(np.float32)


def halves(matrix):
    top = matrix.astype(ml_dtypes.bfloat16)
    return top, (matrix - top.astype(np.float32)).astype(ml_dtypes.bfloat16)


def split(value):
    top = value.astype(jnp.bfloat16)
    return top, (value - top.astype(jnp.float32)).astype(jnp.bfloat16)


def dot(left, right):
    return jnp.dot(left, right, preferred_element_type=jnp.float32)


def rows_times(value, table):
    width = table.shape[1] // 2
    top, rest = split(value)
    both = dot(top, table)
    return both[:, :width] + both[:, width:] + dot(rest, table[:, :width])


def kernel(
    rows, columns, velocity, third, first, second, filtered, stress,
    fine, lines, send_a, recv_a, send_b, recv_b, send_c, recv_c,
    load_sem, send_a_sem, recv_a_sem, send_b_sem, recv_b_sem, send_c_sem, recv_c_sem,
):
    me_y = lax.axis_index("py")
    me_z = lax.axis_index("pz")
    _, _, blocks, near, fine_points = fine.shape
    depth = rows * blocks
    block, band = M // columns, M // rows
    share = block // rows
    slots = send_b.shape[0]
    MESH = pl.DeviceIdType.MESH

    for c in range(3):

        def load(b, carry):
            pltpu.make_async_copy(
                velocity.at[c, :, b, :], fine.at[c, b % rows, b // rows], load_sem.at[c]
            ).start()
            return carry

        lax.fori_loop(0, depth, load, 0)

    barrier = pltpu.get_barrier_semaphore()
    for k in range(1, columns):
        pl.semaphore_signal(
            barrier, inc=1, device_id=(me_y, (me_z + k) % columns), device_id_type=MESH
        )
    for j in range(1, rows):
        pl.semaphore_signal(
            barrier, inc=1, device_id=((me_y + j) % rows, me_z), device_id_type=MESH
        )
    pl.semaphore_wait(barrier, columns + rows - 2)

    def copy_a(f, j):
        return pltpu.make_async_remote_copy(
            src_ref=send_a.at[f, j - 1],
            dst_ref=recv_a.at[f, :, pl.ds(pl.multiple_of(me_y * near, 8), near)],
            send_sem=send_a_sem.at[f, j - 1],
            recv_sem=recv_a_sem.at[f, j - 1],
            device_id=((me_y + j) % rows, me_z),
            device_id_type=MESH,
        )

    def copy_b(f, k):
        return pltpu.make_async_remote_copy(
            src_ref=send_b.at[f % slots, pl.ds((me_z + k) % columns * share, share)],
            dst_ref=recv_b.at[f, :, pl.ds(pl.multiple_of(me_z * depth, 8), depth)],
            send_sem=send_b_sem.at[f, k - 1],
            recv_sem=recv_b_sem.at[f, k - 1],
            device_id=(me_y, (me_z + k) % columns),
            device_id_type=MESH,
        )

    def copy_c(f, j):
        return pltpu.make_async_remote_copy(
            src_ref=send_c.at[f, (me_y + j) % rows],
            dst_ref=recv_c.at[f, pl.ds(me_y, 1)],
            send_sem=send_c_sem.at[f, j - 1],
            recv_sem=recv_c_sem.at[f, j - 1],
            device_id=((me_y + j) % rows, me_z),
            device_id_type=MESH,
        )

    def pair_of(f):
        return f // 6 + f // 8, f - 3 - 2 * (f // 6) - f // 8

    def contract_third(f, product):
        if product:
            left, right = pair_of(f)
        else:
            left = right = f

        def piece(r, carry):
            value = fine[left, r]
            if product:
                value = value * fine[right, r]
            value = value.reshape(blocks * near, fine_points)
            lines[r] = rows_times(value, third[r]).reshape(blocks, near, LANES)
            return carry

        lax.fori_loop(0, rows, piece, 0)

        group = lax.broadcasted_iota(jnp.int32, (near, LANES), 1) % rows
        masks = [group == (me_y + r) % rows for r in range(rows)]

        def regroup(q, carry):
            parts = [lines[r, q] for r in range(rows)]
            for j in range(rows):
                out = parts[-1]
                for r in range(rows - 1):
                    out = jnp.where(masks[(j + r) % rows], parts[r], out)
                if j == 0:
                    recv_a[f, q, pl.ds(pl.multiple_of(me_y * near, 8), near)] = out
                else:
                    send_a[f, j - 1, q] = out
            return carry

        lax.fori_loop(0, blocks, regroup, 0)
        for j in range(1, rows):
            copy_a(f, j).start()

    def table_times(table, value):
        top, rest = split(value)
        both = dot(table, top)
        return both[:M] + both[M:] + dot(table[:M], rest)

    def contract_first(f, reuse):
        for j in range(1, rows):
            copy_a(f, j).wait_recv()
        if reuse:
            for k in range(1, columns):
                copy_b(f - slots, k).wait_send()
        slot = f % slots

        def piece(h, carry):
            value = jnp.concatenate([recv_a[f, 2 * h + i] for i in range(2)], axis=1)
            out = table_times(first[...], value)
            for i in range(2):
                turned = out[:, i * LANES : (i + 1) * LANES].T.reshape(M // rows, rows, M)
                send_b[slot, :, pl.ds(pl.multiple_of((2 * h + i) * rows, 8), rows)] = turned
            return carry

        lax.fori_loop(0, blocks // 2, piece, 0)
        for k in range(1, columns):
            copy_b(f, k).start()
        recv_b[f, :, pl.ds(pl.multiple_of(me_z * depth, 8), depth)] = send_b[
            slot, pl.ds(me_z * share, share)
        ]

    def contract_second(f):
        for k in range(1, columns):
            copy_b(f, k).wait_recv()
        for h in range(share // 2):
            value = jnp.concatenate([recv_b[f, 2 * h + i] for i in range(2)], axis=1)
            out = table_times(second[...], value)
            for i in range(2):
                part = out[:, i * LANES : (i + 1) * LANES]
                for d in range(rows):
                    send_c[f, d, 0, 2 * h + i] = part[d * band : (d + 1) * band]
        for j in range(1, rows):
            copy_c(f, j).start()
        recv_c[f, me_y] = send_c[f, me_y, 0]

    def place(f, product):
        for j in range(1, rows):
            copy_c(f, j).wait_recv()
        whole = recv_c.at[f].reshape(rows * share * band, M)

        def line(m, carry):
            out = whole[pl.ds(m, block, stride=band), :]
            if product:
                left, right = pair_of(f)
                stress[f - 3, m] = out - filtered[left, m] * filtered[right, m]
            else:
                filtered[f, m] = out
            return carry

        lax.fori_loop(0, band, line, 0)

    def loop(start, stop, *work):
        def body(f, carry):
            for one in work:
                one(f)
            return carry

        lax.fori_loop(start, stop, body, 0)

    def loaded(c):
        pltpu.make_async_copy(fine.at[c], fine.at[c], load_sem.at[c]).wait()

    loop(0, 3, loaded, lambda f: contract_third(f, False))
    loop(3, fields_count, lambda f: contract_third(f, True))
    loop(0, 2, lambda f: contract_first(f, False))
    loop(2, slots, lambda f: contract_first(f, False), lambda f: contract_second(f - 2))
    loop(slots, fields_count, lambda f: contract_first(f, True), lambda f: contract_second(f - 2))
    loop(fields_count - 2, fields_count, contract_second)
    loop(0, 3, lambda f: place(f, False))
    loop(3, fields_count, lambda f: place(f, True))

    def finish(f):
        for j in range(1, rows):
            copy_a(f, j).wait_send()
            copy_c(f, j).wait_send()

    loop(0, fields_count, finish)

    def drain(f):
        for k in range(1, columns):
            copy_b(f, k).wait_send()

    loop(fields_count - slots, fields_count, drain)


def tables(fine, rows, columns):
    matrix = line_filter(fine, M)
    depth = fine // columns
    block = M // columns
    share = block // rows
    top, rest = halves(matrix)
    spot, group = np.arange(M) // rows, np.arange(M) % rows
    third = []
    for r in range(rows):
        order = spot // share * block + (group - r) % rows * share + spot % share
        third.append(np.concatenate([top.T[:, order], rest.T[:, order]], axis=1))
    first = np.concatenate([top, rest])
    second = []
    point = np.arange(fine)
    for y in range(rows):
        order = point // rows * rows + (point - y) % rows
        second.append(np.concatenate([top[:, order], rest[:, order]]))
    return np.stack(third), first, np.stack(second)


def kernel_shards(velocity):
    rows, columns = lax.axis_size("py"), lax.axis_size("pz")
    me_y = lax.axis_index("py")
    _, near, depth, fine = velocity.shape
    blocks = depth // rows
    block, band = M // columns, M // rows
    share = block // rows
    slots = 3
    third, first, second = tables(fine, rows, columns)
    second = lax.dynamic_slice(jnp.asarray(second), (me_y, 0, 0), (1, 2 * M, fine))[0]
    vmem = pl.BlockSpec(memory_space=pltpu.VMEM)
    dma = pltpu.SemaphoreType.DMA
    f32 = jnp.float32
    return pl.pallas_call(
        functools.partial(kernel, rows, columns),
        out_shape=(
            jax.ShapeDtypeStruct((3, band, block, M), f32),
            jax.ShapeDtypeStruct((6, band, block, M), f32),
        ),
        in_specs=[pl.BlockSpec(memory_space=pl.ANY), vmem, vmem, vmem],
        out_specs=(vmem, vmem),
        scratch_shapes=[
            pltpu.VMEM((3, rows, blocks, near, fine), f32),
            pltpu.VMEM((rows, blocks, near, LANES), f32),
            pltpu.VMEM((fields_count, rows - 1, blocks, near, LANES), f32),
            pltpu.VMEM((fields_count, blocks, rows * near, LANES), f32),
            pltpu.VMEM((slots, columns * share, depth, M), f32),
            pltpu.VMEM((fields_count, share, columns * depth, M), f32),
            pltpu.VMEM((fields_count, rows, 1, share, band, M), f32),
            pltpu.VMEM((fields_count, rows, share, band, M), f32),
            dma((3,)),
            dma((fields_count, rows - 1)),
            dma((fields_count, rows - 1)),
            dma((fields_count, columns - 1)),
            dma((fields_count, columns - 1)),
            dma((fields_count, rows - 1)),
            dma((fields_count, rows - 1)),
        ],
        compiler_params=pltpu.CompilerParams(
            collective_id=0, has_side_effects=True, vmem_limit_bytes=67_000_000
        ),
    )(velocity, jnp.asarray(third), jnp.asarray(first), second)


def plain_shards(velocity):
    matrix = jnp.asarray(line_filter(velocity.shape[3], M))
    components = [velocity[component] for component in range(3)]
    fields = jnp.stack(components + [components[a] * components[b] for a, b in factor_pairs])
    high = lax.Precision.HIGHEST
    third = jnp.einsum("fabk,mk->fabm", fields, matrix, precision=high)
    third = lax.all_to_all(third, "pz", split_axis=3, concat_axis=2, tiled=True)
    second = jnp.einsum("fabm,nb->fanm", third, matrix, precision=high)
    second = lax.all_to_all(second, "py", split_axis=2, concat_axis=1, tiled=True)
    coarse = jnp.einsum("fanm,pa->fnmp", second, matrix, precision=high)
    stress = jnp.stack(
        [coarse[3 + p] - coarse[a] * coarse[b] for p, (a, b) in enumerate(factor_pairs)]
    )
    return coarse[:3], stress


def shards(velocity):
    rows, columns = lax.axis_size("py"), lax.axis_size("pz")
    _, lines, depth, fine = velocity.shape
    whole_tiles = (
        M == LANES
        and rows % 8 == 0
        and lines % 8 == 0
        and depth % (2 * rows) == 0
        and M % (2 * rows * columns) == 0
        and (M // rows) % 8 == 0
    )
    return kernel_shards(velocity) if whole_tiles else plain_shards(velocity)


def solution(mesh):
    placed = P(None, "py", "pz", None)
    return jax.shard_map(
        shards, mesh=mesh, in_specs=(placed,), out_specs=(placed, placed), check_vma=False
    )
```

time: 342 us -> 211 us (0.62)
  Pallas kernels: 334 us -> 205 us
    pallas_call x1, Pallas kernels: 334 us -> 205 us  [kernel_shards(): pl.pallas_call(functools.partial(kernel, rows, columns), out_shape=(jax.S...]
where the time goes in v1:
time: 211 us
  Pallas kernels  205 us (97%)
  local copies, waits for them, and re-layouts  4.96 us (2%)
    pallas_call x1, Pallas kernels, kernel_shards(): pl.pallas_call(functools.partial(kernel, rows, columns), out_shape=(jax.S...  205 us

profile of v1, /device:TPU:0, one launch (start us, length us, event | category | flops | bytes accessed | tf_op | source)
XLA Modules:
  0.0 210.5 jit_solution(17609587194567330905)
XLA Ops:
  0.6 1.6 dynamic-slice_bitcast_fusion.second
  2.3 204.9 %shard_map.59 = (f32[3,16,32,128]{3,2,1,0:T(8,128)}, f32[6,16,32,128]{3,2,1,0:T(8,128)}) custom-call(f32[3,40,80,320]{3,2,1,0:T(8,128)} %velocity.1, bf16[8,320,256]{2,1,0:T(8,128)(2,1)} %constant.17.clone.third, bf16[256,320]{1,0:T(8,128)(2,1)} %constant.18.clone.first, bf16[256,320]{1,0:T(8,128)(2,1)} %dynamic-slice_bitcast_fusion.second), custom_call_target="tpu_custom_call" | custom-call | tf_op jit(solution)/shard_map/pallas_call | solution.py:282
  207.2 0.0 copy-start
  207.2 2.2 %copy.8 = f32[3,16,32,128]{3,2,1,0:T(8,128)} copy(f32[3,16,32,128]{3,2,1,0:T(8,128)} %get-tuple-element.4) | data formatting | bytes 1572864
  209.4 0.0 copy-done
  209.4 1.1 copy.9
Async XLA Ops:
  207.2 2.2 %copy-start = (f32[6,16,32,128]{3,2,1,0:T(8,128)S(1)}, f32[6,16,32,128]{3,2,1,0:T(8,128)}, u32[]{:S(2)}) copy-start(f32[6,16,32,128]{3,2,1,0:T(8,128)} %get-tuple-element.5) | copy-start | bytes 4718596

commit v2 on v1

v2 whole, which is shorter than its diff:
```python
import functools
import math

import jax
import jax.numpy as jnp
import ml_dtypes
import numpy as np
from jax import lax
from jax.experimental import pallas as pl
from jax.experimental.pallas import tpu as pltpu
from jax.sharding import PartitionSpec as P

M = 128

factor_pairs = ((0, 0), (0, 1), (0, 2), (1, 1), (1, 2), (2, 2))
fields_count = 9
LANES = 128


def line_filter(fine, coarse):
    half = coarse // 2
    modes = np.arange(1, half)
    width = 2.0 * math.pi / coarse
    gain = np.exp(-(modes.astype(np.float64) ** 2) * (width * width / 24.0))
    turns = np.arange(coarse)[:, None] * fine - np.arange(fine)[None, :] * coarse
    period = fine * coarse
    matrix = np.ones((coarse, fine))
    for mode, weight in zip(modes, gain):
        matrix += 2.0 * weight * np.cos(2.0 * math.pi * ((mode * turns) % period) / period)
    return (matrix / fine).astype(np.float32)


def halves(matrix):
    top = matrix.astype(ml_dtypes.bfloat16)
    return top, (matrix - top.astype(np.float32)).astype(ml_dtypes.bfloat16)


def split(value):
    top = value.astype(jnp.bfloat16)
    return top, (value - top.astype(jnp.float32)).astype(jnp.bfloat16)


def dot(left, right):
    return jnp.dot(left, right, preferred_element_type=jnp.float32)


def rows_times(value, table):
    width = table.shape[1] // 2
    top, rest = split(value)
    both = dot(top, table)
    return both[:, :width] + both[:, width:] + dot(rest, table[:, :width])


def flip(me, bits):
    out, weight = me, 1
    while weight <= bits:
        if bits & weight:
            out = out + weight - 2 * weight * (me // weight % 2)
        weight *= 2
    return out


def flip_by(value, bits, rows):
    out, weight = value, 1
    while weight < rows:
        bit = bits // weight % 2
        out = out + bit * (weight - 2 * weight * (value // weight % 2))
        weight *= 2
    return out


def spread(rows, mode):
    step = rows // 2 if mode == 0 else rows // 4
    return step, [(j, j // step % 2, j // (2 * step) * step + j % step) for j in range(rows)]


def kernel(
    rows, columns, velocity, third_table, first_table, base_table, filtered, stress,
    third, first, base, second, fine, lines, send_a, recv_a, send_p, recv_p, send_b, recv_b, send_c, recv_c,
    table_sem, load_sem, send_a_sem, recv_a_sem, send_p_sem, recv_p_sem,
    send_b_sem, recv_b_sem, send_c_sem, recv_c_sem,
):
    me_y = lax.axis_index("py")
    me_z = lax.axis_index("pz")
    _, _, blocks, near, fine_points = fine.shape
    depth = rows * blocks
    block, band = M // columns, M // rows
    share = block // rows
    slots_a, slots_p, slots_b = send_a.shape[0], send_p.shape[0], send_b.shape[0]
    MESH = pl.DeviceIdType.MESH

    steps_of = [spread(rows, mode)[0] for mode in range(2)]
    table_copies = [
        pltpu.make_async_copy(third_table, third, table_sem.at[0]),
        pltpu.make_async_copy(base_table, base, table_sem.at[1]),
    ] + [
        pltpu.make_async_copy(
            first_table.at[mode, me_y // steps_of[mode] % 2], first.at[mode], table_sem.at[2 + mode]
        )
        for mode in range(2)
    ]
    for copy in table_copies:
        copy.start()

    for c in range(3):

        def load(b, carry):
            pltpu.make_async_copy(
                velocity.at[c, :, b, :], fine.at[c, b % rows, b // rows], load_sem.at[c]
            ).start()
            return carry

        lax.fori_loop(0, depth, load, 0)

    barrier = pltpu.get_barrier_semaphore()
    for k in range(1, columns):
        pl.semaphore_signal(
            barrier, inc=1, device_id=(me_y, (me_z + k) % columns), device_id_type=MESH
        )
    for j in range(1, rows):
        pl.semaphore_signal(barrier, inc=1, device_id=(flip(me_y, j), me_z), device_id_type=MESH)
    pl.semaphore_wait(barrier, columns + rows - 2)

    def own_lines(mode):
        step = steps_of[mode]
        at = me_y // (2 * step) * step + me_y % step
        return pl.ds(pl.multiple_of(at * near, 8), near)

    def copies_a(f, mode, side):
        step, tiles = spread(rows, mode)
        return [
            pltpu.make_async_remote_copy(
                src_ref=send_a.at[f % slots_a, side, u - 1],
                dst_ref=recv_a.at[f, side, :, own_lines(mode)],
                send_sem=send_a_sem.at[f, side, u - 1],
                recv_sem=recv_a_sem.at[f, side, u - 1],
                device_id=(flip(me_y, j - side * step), me_z),
                device_id_type=MESH,
            )
            for j, s, u in tiles
            if s == side and u > 0
        ]

    def copy_p(f, mode):
        step, _ = spread(rows, mode)
        return pltpu.make_async_remote_copy(
            src_ref=send_p.at[f % slots_p],
            dst_ref=recv_p.at[f],
            send_sem=send_p_sem.at[f],
            recv_sem=recv_p_sem.at[f],
            device_id=(flip(me_y, step), me_z),
            device_id_type=MESH,
        )

    def copy_b(f, k):
        return pltpu.make_async_remote_copy(
            src_ref=send_b.at[f % slots_b, pl.ds((me_z + k) % columns * share, share)],
            dst_ref=recv_b.at[f, :, pl.ds(pl.multiple_of(me_z * depth, 8), depth)],
            send_sem=send_b_sem.at[f, k - 1],
            recv_sem=recv_b_sem.at[f, k - 1],
            device_id=(me_y, (me_z + k) % columns),
            device_id_type=MESH,
        )

    def copy_c(f, j):
        return pltpu.make_async_remote_copy(
            src_ref=send_c.at[f, pl.ds(flip(me_y, j), 1)],
            dst_ref=recv_c.at[f, pl.ds(me_y, 1)],
            send_sem=send_c_sem.at[f, j - 1],
            recv_sem=recv_c_sem.at[f, j - 1],
            device_id=(flip(me_y, j), me_z),
            device_id_type=MESH,
        )

    def pair_of(f):
        return f // 6 + f // 8, f - 3 - 2 * (f // 6) - f // 8

    group = lax.broadcasted_iota(jnp.int32, (near, LANES), 1) % rows

    def contract_third(f, mode):
        product = f >= 3
        left, right = pair_of(f)
        left = jnp.where(product, left, f)
        right = jnp.where(product, right, f)

        def piece(r, carry):
            value = fine[left, r] * jnp.where(product, fine[right, r], 1.0)
            value = value.reshape(blocks * near, fine_points)
            lines[r] = rows_times(value, third[r]).reshape(blocks, near, LANES)
            return carry

        lax.fori_loop(0, rows, piece, 0)
        masks = [group == flip(me_y, r) for r in range(rows)]
        _, tiles = spread(rows, mode)

        def regroup(q, carry):
            parts = [lines[r, q] for r in range(rows)]
            for j, side, u in tiles:
                out = parts[-1]
                for r in range(rows - 1):
                    out = jnp.where(masks[j ^ r], parts[r], out)
                if u == 0:
                    recv_a[f, side, q, own_lines(mode)] = out
                else:
                    send_a[f % slots_a, side, u - 1, q] = out
            return carry

        lax.fori_loop(0, blocks, regroup, 0)
        for side in (1, 0):
            for copy in copies_a(f, mode, side):
                copy.start()

    def free_a(f, mode):
        for side in (1, 0):
            for copy in copies_a(f, mode, side):
                copy.wait_send()

    def table_times(table, value):
        top, rest = split(value)
        both = dot(table, top)
        return both[:M] + both[M:] + dot(table[:M], rest)

    def partial_first(f, mode, side, h):
        value = jnp.concatenate([recv_a[f, side, 2 * h + i] for i in range(2)], axis=1)
        return table_times(first[mode], value)

    def first_out(f, mode):
        for copy in copies_a(f, mode, 1):
            copy.wait_recv()

        @pl.when(f >= slots_p)
        def _():
            copy_p(f - slots_p, mode).wait_send()

        def piece(h, carry):
            out = partial_first(f, mode, 1, h)
            for i in range(2):
                send_p[f % slots_p, 2 * h + i] = out[:, i * LANES : (i + 1) * LANES]
            return carry

        lax.fori_loop(0, blocks // 2, piece, 0)
        copy_p(f, mode).start()

    def first_in(f, mode):
        for copy in copies_a(f, mode, 0):
            copy.wait_recv()
        copy_p(f, mode).wait_recv()

        @pl.when(f >= slots_b)
        def _():
            for k in range(1, columns):
                copy_b(f - slots_b, k).wait_send()

        slot = f % slots_b

        def piece(h, carry):
            out = partial_first(f, mode, 0, h)
            for i in range(2):
                part = out[:, i * LANES : (i + 1) * LANES] + recv_p[f, 2 * h + i]
                send_b[slot, :, pl.ds(pl.multiple_of((2 * h + i) * rows, 8), rows)] = (
                    part.T.reshape(M // rows, rows, M)
                )
            return carry

        lax.fori_loop(0, blocks // 2, piece, 0)
        for k in range(1, columns):
            copy_b(f, k).start()
        recv_b[f, :, pl.ds(pl.multiple_of(me_z * depth, 8), depth)] = send_b[
            slot, pl.ds(me_z * share, share)
        ]

    def contract_second(f):
        for k in range(1, columns):
            copy_b(f, k).wait_recv()
        for h in range(share // 2):
            value = jnp.concatenate([recv_b[f, 2 * h + i] for i in range(2)], axis=1)
            out = table_times(second[...], value)
            for i in range(2):
                part = out[:, i * LANES : (i + 1) * LANES]
                for d in range(rows):
                    send_c[f, d, 2 * h + i] = part[d * band : (d + 1) * band]
        for j in range(1, rows):
            copy_c(f, j).start()
        recv_c[f, me_y] = send_c[f, me_y]

    def place(f, product):
        for j in range(1, rows):
            copy_c(f, j).wait_recv()
        whole = recv_c.at[f].reshape(rows * share * band, M)

        def line(m, carry):
            out = whole[pl.ds(m, block, stride=band), :]
            if product:
                left, right = pair_of(f)
                stress[f - 3, m] = out - filtered[left, m] * filtered[right, m]
            else:
                filtered[f, m] = out
            return carry

        lax.fori_loop(0, band, line, 0)

    def loop(start, stop, *work):
        def body(f, carry):
            for one in work:
                one(f)
            return carry

        lax.fori_loop(start, stop, body, 0)

    def loaded(c):
        pltpu.make_async_copy(fine.at[c], fine.at[c], load_sem.at[c]).wait()

    for copy in table_copies:
        copy.wait()

    for f in range(slots_a):
        if f < 3:
            loaded(f)
        contract_third(f, f % 2)

    points = base.shape[1]
    row = lax.broadcasted_iota(jnp.int32, (points, points), 0)
    column = lax.broadcasted_iota(jnp.int32, (points, points), 1)
    swap = jnp.where(row == flip_by(column, me_y, rows), 1.0, 0.0).astype(jnp.bfloat16)
    second[...] = dot(base[...], swap).astype(jnp.bfloat16)

    def steps(g):
        for mode in range(2):
            f = 2 * g + mode

            @pl.when(f < fields_count)
            def _():
                first_out(f, mode)

            @pl.when(f + slots_a < fields_count)
            def _():
                free_a(f, mode)
                contract_third(f + slots_a, mode)

            @pl.when((f >= 1) & (f <= fields_count))
            def _():
                first_in(f - 1, 1 - mode)

            @pl.when((f >= 2) & (f <= fields_count + 1))
            def _():
                contract_second(f - 2)

    loop(0, (fields_count + 3) // 2, steps)
    loop(0, 3, lambda f: place(f, False))
    loop(3, fields_count, lambda f: place(f, True))

    for f in range(fields_count - slots_a, fields_count):
        free_a(f, f % 2)
    for f in range(fields_count - slots_p, fields_count):
        copy_p(f, f % 2).wait_send()
    for f in range(fields_count - slots_b, fields_count):
        for k in range(1, columns):
            copy_b(f, k).wait_send()

    def finish(f):
        for j in range(1, rows):
            copy_c(f, j).wait_send()

    loop(0, fields_count, finish)


def tables(fine, rows, columns):
    matrix = line_filter(fine, M)
    block = M // columns
    share = block // rows
    near = fine // rows
    top, rest = halves(matrix)
    both = np.concatenate([top, rest])
    spot, group = np.arange(M) // rows, np.arange(M) % rows
    third = []
    for r in range(rows):
        order = spot // share * block + (group ^ r) * share + spot % share
        third.append(np.concatenate([top.T[:, order], rest.T[:, order]], axis=1))
    first = []
    for mode in range(2):
        step, _ = spread(rows, mode)
        spots = np.arange(rows // 2)
        for half in range(2):
            peers = spots // step * (2 * step) + half * step + spots % step
            order = (peers[:, None] * near + np.arange(near)).reshape(-1)
            first.append(both[:, order])
    return np.stack(third), np.stack(first).reshape(2, 2, 2 * M, fine // 2), both


def kernel_shards(velocity):
    rows, columns = lax.axis_size("py"), lax.axis_size("pz")
    _, near, depth, fine = velocity.shape
    blocks = depth // rows
    block, band = M // columns, M // rows
    share = block // rows
    half = rows // 2
    slots_a, slots_p, slots_b = 4, 2, 3
    third, first, base = tables(fine, rows, columns)
    vmem = pl.BlockSpec(memory_space=pltpu.VMEM)
    dma = pltpu.SemaphoreType.DMA
    f32 = jnp.float32
    return pl.pallas_call(
        functools.partial(kernel, rows, columns),
        out_shape=(
            jax.ShapeDtypeStruct((3, band, block, M), f32),
            jax.ShapeDtypeStruct((6, band, block, M), f32),
        ),
        in_specs=[pl.BlockSpec(memory_space=pl.ANY)] * 4,
        out_specs=(vmem, vmem),
        scratch_shapes=[
            pltpu.VMEM(third.shape, jnp.bfloat16),
            pltpu.VMEM(first.shape[1:], jnp.bfloat16),
            pltpu.VMEM(base.shape, jnp.bfloat16),
            pltpu.VMEM(base.shape, jnp.bfloat16),
            pltpu.VMEM((3, rows, blocks, near, fine), f32),
            pltpu.VMEM((rows, blocks, near, LANES), f32),
            pltpu.VMEM((slots_a, 2, half - 1, blocks, near, LANES), f32),
            pltpu.VMEM((fields_count, 2, blocks, half * near, LANES), f32),
            pltpu.VMEM((slots_p, blocks, M, LANES), f32),
            pltpu.VMEM((fields_count, blocks, M, LANES), f32),
            pltpu.VMEM((slots_b, columns * share, depth, M), f32),
            pltpu.VMEM((fields_count, share, columns * depth, M), f32),
            pltpu.VMEM((fields_count, rows, share, band, M), f32),
            pltpu.VMEM((fields_count, rows, share, band, M), f32),
            dma((4,)),
            dma((3,)),
            dma((fields_count, 2, half - 1)),
            dma((fields_count, 2, half - 1)),
            dma((fields_count,)),
            dma((fields_count,)),
            dma((fields_count, columns - 1)),
            dma((fields_count, columns - 1)),
            dma((fields_count, rows - 1)),
            dma((fields_count, rows - 1)),
        ],
        compiler_params=pltpu.CompilerParams(
            collective_id=0, has_side_effects=True, vmem_limit_bytes=67_000_000
        ),
    )(velocity, jnp.asarray(third), jnp.asarray(first), jnp.asarray(base))


def plain_shards(velocity):
    matrix = jnp.asarray(line_filter(velocity.shape[3], M))
    components = [velocity[component] for component in range(3)]
    fields = jnp.stack(components + [components[a] * components[b] for a, b in factor_pairs])
    high = lax.Precision.HIGHEST
    third = jnp.einsum("fabk,mk->fabm", fields, matrix, precision=high)
    third = lax.all_to_all(third, "pz", split_axis=3, concat_axis=2, tiled=True)
    second = jnp.einsum("fabm,nb->fanm", third, matrix, precision=high)
    second = lax.all_to_all(second, "py", split_axis=2, concat_axis=1, tiled=True)
    coarse = jnp.einsum("fanm,pa->fnmp", second, matrix, precision=high)
    stress = jnp.stack(
        [coarse[3 + p] - coarse[a] * coarse[b] for p, (a, b) in enumerate(factor_pairs)]
    )
    return coarse[:3], stress


def shards(velocity):
    rows, columns = lax.axis_size("py"), lax.axis_size("pz")
    _, lines, depth, fine = velocity.shape
    whole_tiles = (
        M == LANES
        and rows % 8 == 0
        and rows & (rows - 1) == 0
        and lines % 8 == 0
        and depth % (2 * rows) == 0
        and M % (2 * rows * columns) == 0
        and (M // rows) % 8 == 0
    )
    return kernel_shards(velocity) if whole_tiles else plain_shards(velocity)


def solution(mesh):
    placed = P(None, "py", "pz", None)
    return jax.shard_map(
        shards, mesh=mesh, in_specs=(placed,), out_specs=(placed, placed), check_vma=False
    )
```

time: 211 us -> 224 us (1.062)
  Pallas kernels: 205 us -> 220 us
    pallas_call x1, Pallas kernels: 205 us -> 220 us  [kernel_shards(): pl.pallas_call(functools.partial(kernel, rows, columns), out_shape=(jax.S...]
where the time goes in v2:
time: 224 us
  Pallas kernels  220 us (98%)
  local copies, waits for them, and re-layouts  3.33 us (1%)
    pallas_call x1, Pallas kernels, kernel_shards(): pl.pallas_call(functools.partial(kernel, rows, columns), out_shape=(jax.S...  220 us

profile of v2, /device:TPU:0, one launch (start us, length us, event | category | flops | bytes accessed | tf_op | source)
XLA Modules:
  0.0 223.7 jit_solution(8440123923241083176)
XLA Ops:
  0.6 219.7 %shard_map.59 = (f32[3,16,32,128]{3,2,1,0:T(8,128)}, f32[6,16,32,128]{3,2,1,0:T(8,128)}) custom-call(f32[3,40,80,320]{3,2,1,0:T(8,128)} %velocity.1, bf16[8,320,256]{2,1,0:T(8,128)(2,1)} %constant.6.clone.third_table, bf16[2,2,256,160]{3,2,1,0:T(8,128)(2,1)} %constant.7.clone.first_table, bf16[256,320]{1,0:T(8,128)(2,1)} %constant.8.clone.base_table), custom_call_target="tpu_custom_call" | custom-call | tf_op jit(solution)/shard_map/pallas_call | solution.py:402
  220.4 0.0 copy-start
  220.4 2.2 copy.8
  222.6 0.0 copy-done
  222.6 1.1 copy.9
Async XLA Ops:
  220.4 2.2 copy-start

commit v3 on v2

v3 whole, which is shorter than its diff:
```python
import functools
import math

import jax
import jax.numpy as jnp
import ml_dtypes
import numpy as np
from jax import lax
from jax.experimental import pallas as pl
from jax.experimental.pallas import tpu as pltpu
from jax.sharding import PartitionSpec as P

M = 128

factor_pairs = ((0, 0), (0, 1), (0, 2), (1, 1), (1, 2), (2, 2))
fields_count = 9
LANES = 128


def line_filter(fine, coarse):
    half = coarse // 2
    modes = np.arange(1, half)
    width = 2.0 * math.pi / coarse
    gain = np.exp(-(modes.astype(np.float64) ** 2) * (width * width / 24.0))
    turns = np.arange(coarse)[:, None] * fine - np.arange(fine)[None, :] * coarse
    period = fine * coarse
    matrix = np.ones((coarse, fine))
    for mode, weight in zip(modes, gain):
        matrix += 2.0 * weight * np.cos(2.0 * math.pi * ((mode * turns) % period) / period)
    return (matrix / fine).astype(np.float32)


def halves(matrix):
    top = matrix.astype(ml_dtypes.bfloat16)
    return top, (matrix - top.astype(np.float32)).astype(ml_dtypes.bfloat16)


def split(value):
    top = value.astype(jnp.bfloat16)
    return top, (value - top.astype(jnp.float32)).astype(jnp.bfloat16)


def dot(left, right):
    return jnp.dot(left, right, preferred_element_type=jnp.float32)


def rows_times(value, table):
    width = table.shape[1] // 2
    top, rest = split(value)
    both = dot(top, table)
    return both[:, :width] + both[:, width:] + dot(rest, table[:, :width])


def flip(me, bits):
    out, weight = me, 1
    while weight <= bits:
        if bits & weight:
            out = out + weight - 2 * weight * (me // weight % 2)
        weight *= 2
    return out


def flip_by(value, bits, rows):
    out, weight = value, 1
    while weight < rows:
        bit = bits // weight % 2
        out = out + bit * (weight - 2 * weight * (value // weight % 2))
        weight *= 2
    return out


def spread(rows, mode):
    step = rows // 2 if mode == 0 else rows // 4
    return step, [(j, j // step % 2, j // (2 * step) * step + j % step) for j in range(rows)]


def kernel(
    rows, columns, velocity, third_table, first_table, base_table, direct_third_table,
    direct_first_table, filtered, stress,
    third, first, base, second, direct_third, direct_first, fine, lines,
    send_a, recv_a, send_p, recv_p, send_b, recv_b, send_c, recv_c,
    natural, direct_lines, send_z, recv_z, send_y, recv_y, turned,
    table_sem, load_sem, natural_sem, send_a_sem, recv_a_sem, send_p_sem, recv_p_sem,
    send_b_sem, recv_b_sem, send_c_sem, recv_c_sem,
    send_z_sem, recv_z_sem, send_y_sem, recv_y_sem,
):
    me_y = lax.axis_index("py")
    me_z = lax.axis_index("pz")
    _, _, blocks, near, fine_points = fine.shape
    depth = rows * blocks
    block, band = M // columns, M // rows
    share = block // rows
    part = blocks // 2
    steps = near // columns
    spun = fields_count - 1
    slots_a, slots_p, slots_b = send_a.shape[0], send_p.shape[0], send_b.shape[0]
    MESH = pl.DeviceIdType.MESH

    strides = [spread(rows, mode)[0] for mode in range(2)]
    table_copies = [
        pltpu.make_async_copy(third_table, third, table_sem.at[0]),
        pltpu.make_async_copy(base_table, base, table_sem.at[1]),
        pltpu.make_async_copy(direct_third_table, direct_third, table_sem.at[2]),
        pltpu.make_async_copy(direct_first_table, direct_first, table_sem.at[3]),
    ] + [
        pltpu.make_async_copy(
            first_table.at[mode, me_y // strides[mode] % 2], first.at[mode], table_sem.at[4 + mode]
        )
        for mode in range(2)
    ]
    last_left, last_right = factor_pairs[-1]

    def load_natural(u):
        return pltpu.make_async_copy(
            velocity.at[last_left, pl.ds(u * 2 * columns, 2 * columns)],
            natural.at[u % 2],
            natural_sem.at[u],
        )

    def load(c):
        def line(b, carry):
            pltpu.make_async_copy(
                velocity.at[c, :, b, :], fine.at[c, b % rows, b // rows], load_sem.at[c]
            ).start()
            return carry

        lax.fori_loop(0, depth, line, 0)

    table_copies[0].start()
    load(0)
    for copy in table_copies[1:]:
        copy.start()
    for u in range(2):
        load_natural(u).start()
    load(1)
    load(2)

    barrier = pltpu.get_barrier_semaphore()
    for k in range(1, columns):
        pl.semaphore_signal(
            barrier, inc=1, device_id=(me_y, (me_z + k) % columns), device_id_type=MESH
        )
    for j in range(1, rows):
        pl.semaphore_signal(barrier, inc=1, device_id=(flip(me_y, j), me_z), device_id_type=MESH)
    pl.semaphore_wait(barrier, columns + rows - 2)

    def own_lines(mode):
        step = strides[mode]
        at = me_y // (2 * step) * step + me_y % step
        return pl.ds(pl.multiple_of(at * near, 8), near)

    def copies_a(f, mode, side):
        step, tiles = spread(rows, mode)
        return [
            pltpu.make_async_remote_copy(
                src_ref=send_a.at[f % slots_a, mode, side, u - 1],
                dst_ref=recv_a.at[f, mode, side, :, own_lines(mode)],
                send_sem=send_a_sem.at[f, mode, side, u - 1],
                recv_sem=recv_a_sem.at[f, mode, side, u - 1],
                device_id=(flip(me_y, j - side * step), me_z),
                device_id_type=MESH,
            )
            for j, s, u in tiles
            if s == side and u > 0
        ]

    def copy_p(f, mode):
        return pltpu.make_async_remote_copy(
            src_ref=send_p.at[f % slots_p, mode],
            dst_ref=recv_p.at[f, mode],
            send_sem=send_p_sem.at[f, mode],
            recv_sem=recv_p_sem.at[f, mode],
            device_id=(flip(me_y, strides[mode]), me_z),
            device_id_type=MESH,
        )

    def copy_b(f, mode, k):
        count = part * rows
        at = me_z * depth + mode * count
        return pltpu.make_async_remote_copy(
            src_ref=send_b.at[
                f % slots_b, pl.ds((me_z + k) % columns * share, share), pl.ds(mode * count, count)
            ],
            dst_ref=recv_b.at[f, :, pl.ds(pl.multiple_of(at, 8), count)],
            send_sem=send_b_sem.at[f, mode, k - 1],
            recv_sem=recv_b_sem.at[f, mode, k - 1],
            device_id=(me_y, (me_z + k) % columns),
            device_id_type=MESH,
        )

    def copy_c(f, j):
        return pltpu.make_async_remote_copy(
            src_ref=send_c.at[f, pl.ds(flip(me_y, j), 1)],
            dst_ref=recv_c.at[f, pl.ds(me_y, 1)],
            send_sem=send_c_sem.at[f, j - 1],
            recv_sem=recv_c_sem.at[f, j - 1],
            device_id=(flip(me_y, j), me_z),
            device_id_type=MESH,
        )

    def copy_z(u, k):
        return pltpu.make_async_remote_copy(
            src_ref=send_z.at[k - 1, pl.ds(2 * u, 2)],
            dst_ref=recv_z.at[pl.ds(2 * u, 2), pl.ds(pl.multiple_of(me_z * depth, 8), depth)],
            send_sem=send_z_sem.at[u, k - 1],
            recv_sem=recv_z_sem.at[u, k - 1],
            device_id=(me_y, (me_z + k) % columns),
            device_id_type=MESH,
        )

    def copy_y(j):
        return pltpu.make_async_remote_copy(
            src_ref=send_y.at[flip(me_y, j)],
            dst_ref=recv_y.at[pl.ds(me_y * steps, steps)],
            send_sem=send_y_sem.at[j - 1],
            recv_sem=recv_y_sem.at[j - 1],
            device_id=(flip(me_y, j), me_z),
            device_id_type=MESH,
        )

    def pair_of(f):
        return f // 6 + f // 8, f - 3 - 2 * (f // 6) - f // 8

    def contract_third(f):
        product = f >= 3
        left, right = pair_of(f)
        left = jnp.where(product, left, f)
        right = jnp.where(product, right, f)
        group = lax.broadcasted_iota(jnp.int32, (near, LANES), 1) % rows
        masks = [group == flip(me_y, r) for r in range(rows)]
        for mode in range(2):
            _, tiles = spread(rows, mode)
            where = pl.ds(mode * part, part)

            def piece(r, carry):
                value = fine[left, r, where] * jnp.where(product, fine[right, r, where], 1.0)
                value = value.reshape(part * near, fine_points)
                lines[r] = rows_times(value, third[r]).reshape(part, near, LANES)
                return carry

            lax.fori_loop(0, rows, piece, 0)

            def regroup(q, carry):
                parts = [lines[r, q] for r in range(rows)]
                for j, side, u in tiles:
                    out = parts[-1]
                    for r in range(rows - 1):
                        out = jnp.where(masks[j ^ r], parts[r], out)
                    if u == 0:
                        recv_a[f, mode, side, q, own_lines(mode)] = out
                    else:
                        send_a[f % slots_a, mode, side, u - 1, q] = out
                return carry

            lax.fori_loop(0, part, regroup, 0)
            for side in (1, 0):
                for copy in copies_a(f, mode, side):
                    copy.start()

    def free_a(f):
        for mode in range(2):
            for side in (1, 0):
                for copy in copies_a(f, mode, side):
                    copy.wait_send()

    def table_times(table, value):
        top, rest = split(value)
        both = dot(table, top)
        return both[:M] + both[M:] + dot(table[:M], rest)

    def partial_first(f, mode, side):
        for at in range(0, part, 2):
            spots = range(at, min(at + 2, part))
            value = jnp.concatenate([recv_a[f, mode, side, q] for q in spots], axis=1)
            out = table_times(first[mode], value)
            for i, q in enumerate(spots):
                yield q, out[:, i * LANES : (i + 1) * LANES]

    def first_out(f):
        for mode in range(2):
            for copy in copies_a(f, mode, 1):
                copy.wait_recv()

            @pl.when(f >= slots_p)
            def _():
                copy_p(f - slots_p, mode).wait_send()

            for q, out in partial_first(f, mode, 1):
                send_p[f % slots_p, mode, q] = out
            copy_p(f, mode).start()

    def first_in(f):
        slot = f % slots_b
        for mode in range(2):
            for copy in copies_a(f, mode, 0):
                copy.wait_recv()
            copy_p(f, mode).wait_recv()

            @pl.when(f >= slots_b)
            def _():
                for k in range(1, columns):
                    copy_b(f - slots_b, mode, k).wait_send()

            count = part * rows
            for q, out in partial_first(f, mode, 0):
                out = out + recv_p[f, mode, q]
                send_b[slot, :, pl.ds(mode * count + q * rows, rows)] = out.T.reshape(
                    M // rows, rows, M
                )
            for k in range(1, columns):
                copy_b(f, mode, k).start()
            at = pl.multiple_of(me_z * depth + mode * count, 8)
            recv_b[f, :, pl.ds(at, count)] = send_b[
                slot, pl.ds(me_z * share, share), pl.ds(mode * count, count)
            ]

    def contract_second(f):
        for mode in range(2):
            for k in range(1, columns):
                copy_b(f, mode, k).wait_recv()
        for h in range(share // 2):
            value = jnp.concatenate([recv_b[f, 2 * h + i] for i in range(2)], axis=1)
            out = table_times(second[...], value)
            for i in range(2):
                piece = out[:, i * LANES : (i + 1) * LANES]
                for d in range(rows):
                    send_c[f, d, 2 * h + i] = piece[d * band : (d + 1) * band]
        for j in range(1, rows):
            copy_c(f, j).start()
        recv_c[f, me_y] = send_c[f, me_y]

    def place(f, product):
        for j in range(1, rows):
            copy_c(f, j).wait_recv()
        whole = recv_c.at[f].reshape(rows * share * band, M)

        def line(m, carry):
            out = whole[pl.ds(m, block, stride=band), :]
            if product:
                left, right = pair_of(f)
                stress[f - 3, m] = out - filtered[left, m] * filtered[right, m]
            else:
                filtered[f, m] = out
            return carry

        lax.fori_loop(0, band, line, 0)

    def direct_contract_third():
        group = lax.broadcasted_iota(jnp.int32, (depth, LANES), 1) // block
        masks = [group == (me_z + k) % columns for k in range(columns)]
        units = steps // 2

        def unit(u, carry):
            load_natural(u).wait()

            def piece(s, inner):
                value = jnp.concatenate(
                    [natural[u % 2, i * columns + s] for i in range(2)], axis=0
                )
                value = value * value
                direct_lines[s] = rows_times(value, direct_third[s]).reshape(2, depth, LANES)
                return inner

            lax.fori_loop(0, columns, piece, 0)

            @pl.when(u + 2 < units)
            def _():
                load_natural(u + 2).start()

            for i in range(2):
                parts = [direct_lines[s, i] for s in range(columns)]
                for k in range(columns):
                    out = parts[-1]
                    for s in range(columns - 1):
                        out = jnp.where(masks[(k + s) % columns], parts[s], out)
                    if k == 0:
                        recv_z[2 * u + i, pl.ds(pl.multiple_of(me_z * depth, 8), depth)] = out
                    else:
                        send_z[k - 1, 2 * u + i] = out
            for k in range(1, columns):
                copy_z(u, k).start()
            return carry

        lax.fori_loop(0, units, unit, 0)

    def direct_contract_second():
        def piece(h, carry):
            for k in range(1, columns):
                copy_z(h, k).wait_recv()
            value = jnp.concatenate([recv_z[2 * h + i] for i in range(2)], axis=1)
            out = table_times(base[...], value)
            for i in range(2):
                for d in range(rows):
                    send_y[d, 2 * h + i] = out[
                        d * band : (d + 1) * band, i * LANES : (i + 1) * LANES
                    ]
            return carry

        lax.fori_loop(0, steps // 2, piece, 0)
        for j in range(1, rows):
            copy_y(j).start()
        recv_y[pl.ds(me_y * steps, steps)] = send_y[me_y]

    def direct_contract_first():
        for j in range(1, rows):
            copy_y(j).wait_recv()
        pad = jnp.zeros((LANES - rows * steps, LANES), jnp.float32)
        for m in range(band):
            plane = jnp.concatenate([recv_y[:, m, :], pad], axis=0).T
            for g in range(columns):
                turned[g, m * block : (m + 1) * block] = plane[g * block : (g + 1) * block]
        out = jnp.zeros((band * block, M), jnp.float32)
        for g in range(columns):
            table = direct_first[(g + columns - me_z) % columns]
            out = out + rows_times(turned[g], table)
        out = out.reshape(band, block, M)
        stress[spun - 3] = out - filtered[last_left] * filtered[last_right]

    def loop(start, stop, *work):
        def body(f, carry):
            for one in work:
                one(f)
            return carry

        lax.fori_loop(start, stop, body, 0)

    def loaded(c):
        pltpu.make_async_copy(fine.at[c], fine.at[c], load_sem.at[c]).wait()

    table_copies[0].wait()
    loaded(0)
    contract_third(0)
    for copy in table_copies[1:]:
        copy.wait()
    direct_contract_third()
    loaded(1)
    contract_third(1)
    loaded(2)

    points = base.shape[1]
    row = lax.broadcasted_iota(jnp.int32, (points, points), 0)
    column = lax.broadcasted_iota(jnp.int32, (points, points), 1)
    swap = jnp.where(row == flip_by(column, me_y, rows), 1.0, 0.0).astype(jnp.bfloat16)
    second[...] = dot(base[...], swap).astype(jnp.bfloat16)

    def round_of(f):
        first_out(f)

        @pl.when(f + slots_a < spun)
        def _():
            free_a(f)
            contract_third(f + slots_a)

        @pl.when(f >= 1)
        def _():
            first_in(f - 1)

    loop(0, spun - 1, round_of)
    first_out(spun - 1)
    loop(0, spun - 3, contract_second)
    direct_contract_second()
    first_in(spun - 2)
    contract_second(spun - 3)
    first_in(spun - 1)
    loop(0, 3, lambda f: place(f, False))
    contract_second(spun - 2)
    loop(3, spun - 3, lambda f: place(f, True))
    direct_contract_first()
    contract_second(spun - 1)
    loop(spun - 3, spun, lambda f: place(f, True))

    loop(spun - slots_a, spun, free_a)

    def drain_p(f):
        for mode in range(2):
            copy_p(f, mode).wait_send()

    loop(spun - slots_p, spun, drain_p)

    def drain_b(f):
        for mode in range(2):
            for k in range(1, columns):
                copy_b(f, mode, k).wait_send()

    loop(spun - slots_b, spun, drain_b)

    def drain_c(f):
        for j in range(1, rows):
            copy_c(f, j).wait_send()

    loop(0, spun, drain_c)

    def drain_z(u):
        for k in range(1, columns):
            copy_z(u, k).wait_send()

    loop(0, steps // 2, drain_z)
    for j in range(1, rows):
        copy_y(j).wait_send()


def tables(fine, rows, columns):
    matrix = line_filter(fine, M)
    block = M // columns
    share = block // rows
    near = fine // rows
    steps = near // columns
    top, rest = halves(matrix)
    both = np.concatenate([top, rest])
    spot, group = np.arange(M) // rows, np.arange(M) % rows
    third = []
    for r in range(rows):
        order = spot // share * block + (group ^ r) * share + spot % share
        third.append(np.concatenate([top.T[:, order], rest.T[:, order]], axis=1))
    first = []
    for mode in range(2):
        step, _ = spread(rows, mode)
        spots = np.arange(rows // 2)
        for half in range(2):
            peers = spots // step * (2 * step) + half * step + spots % step
            order = (peers[:, None] * near + np.arange(near)).reshape(-1)
            first.append(both[:, order])
    first = np.stack(first).reshape(2, 2, 2 * M, fine // 2)
    direct_third, direct_first = [], []
    for s in range(columns):
        order = np.concatenate(
            [np.arange(block) + (g - s) % columns * block for g in range(columns)]
        )
        direct_third.append(np.concatenate([top.T[:, order], rest.T[:, order]], axis=1))
        points = np.arange(rows * steps) * columns + s
        table = np.concatenate([top.T[points], rest.T[points]], axis=1)
        direct_first.append(np.pad(table, ((0, LANES - rows * steps), (0, 0))))
    return np.stack(third), first, both, np.stack(direct_third), np.stack(direct_first)


def kernel_shards(velocity):
    rows, columns = lax.axis_size("py"), lax.axis_size("pz")
    _, near, depth, fine = velocity.shape
    blocks = depth // rows
    block, band = M // columns, M // rows
    share = block // rows
    half, part, steps = rows // 2, blocks // 2, near // columns
    spun = fields_count - 1
    slots_a, slots_p, slots_b = 2, 2, 2
    constants = tables(fine, rows, columns)
    third, first, base, direct_third, direct_first = constants
    vmem = pl.BlockSpec(memory_space=pltpu.VMEM)
    dma = pltpu.SemaphoreType.DMA
    f32, bf16 = jnp.float32, jnp.bfloat16
    return pl.pallas_call(
        functools.partial(kernel, rows, columns),
        out_shape=(
            jax.ShapeDtypeStruct((3, band, block, M), f32),
            jax.ShapeDtypeStruct((6, band, block, M), f32),
        ),
        in_specs=[pl.BlockSpec(memory_space=pl.ANY)] * (1 + len(constants)),
        out_specs=(vmem, vmem),
        scratch_shapes=[
            pltpu.VMEM(third.shape, bf16),
            pltpu.VMEM(first.shape[1:], bf16),
            pltpu.VMEM(base.shape, bf16),
            pltpu.VMEM(base.shape, bf16),
            pltpu.VMEM(direct_third.shape, bf16),
            pltpu.VMEM(direct_first.shape, bf16),
            pltpu.VMEM((3, rows, blocks, near, fine), f32),
            pltpu.VMEM((rows, part, near, LANES), f32),
            pltpu.VMEM((slots_a, 2, 2, half - 1, part, near, LANES), f32),
            pltpu.VMEM((spun, 2, 2, part, half * near, LANES), f32),
            pltpu.VMEM((slots_p, 2, part, M, LANES), f32),
            pltpu.VMEM((spun, 2, part, M, LANES), f32),
            pltpu.VMEM((slots_b, columns * share, depth, M), f32),
            pltpu.VMEM((spun, share, columns * depth, M), f32),
            pltpu.VMEM((spun, rows, share, band, M), f32),
            pltpu.VMEM((spun, rows, share, band, M), f32),
            pltpu.VMEM((2, 2 * columns, depth, fine), f32),
            pltpu.VMEM((columns, 2, depth, LANES), f32),
            pltpu.VMEM((columns - 1, steps, depth, LANES), f32),
            pltpu.VMEM((steps, columns * depth, LANES), f32),
            pltpu.VMEM((rows, steps, band, LANES), f32),
            pltpu.VMEM((rows * steps, band, LANES), f32),
            pltpu.VMEM((columns, band * block, LANES), f32),
            dma((6,)),
            dma((3,)),
            dma((steps // 2,)),
            dma((spun, 2, 2, half - 1)),
            dma((spun, 2, 2, half - 1)),
            dma((spun, 2)),
            dma((spun, 2)),
            dma((spun, 2, columns - 1)),
            dma((spun, 2, columns - 1)),
            dma((spun, rows - 1)),
            dma((spun, rows - 1)),
            dma((steps // 2, columns - 1)),
            dma((steps // 2, columns - 1)),
            dma((rows - 1,)),
            dma((rows - 1,)),
        ],
        compiler_params=pltpu.CompilerParams(
            collective_id=0, has_side_effects=True, vmem_limit_bytes=67_000_000
        ),
    )(velocity, *[jnp.asarray(constant) for constant in constants])


def plain_shards(velocity):
    matrix = jnp.asarray(line_filter(velocity.shape[3], M))
    components = [velocity[component] for component in range(3)]
    fields = jnp.stack(components + [components[a] * components[b] for a, b in factor_pairs])
    high = lax.Precision.HIGHEST
    third = jnp.einsum("fabk,mk->fabm", fields, matrix, precision=high)
    third = lax.all_to_all(third, "pz", split_axis=3, concat_axis=2, tiled=True)
    second = jnp.einsum("fabm,nb->fanm", third, matrix, precision=high)
    second = lax.all_to_all(second, "py", split_axis=2, concat_axis=1, tiled=True)
    coarse = jnp.einsum("fanm,pa->fnmp", second, matrix, precision=high)
    stress = jnp.stack(
        [coarse[3 + p] - coarse[a] * coarse[b] for p, (a, b) in enumerate(factor_pairs)]
    )
    return coarse[:3], stress


def shards(velocity):
    rows, columns = lax.axis_size("py"), lax.axis_size("pz")
    _, lines, depth, fine = velocity.shape
    whole_tiles = (
        M == LANES
        and rows % 8 == 0
        and rows & (rows - 1) == 0
        and lines % 8 == 0
        and lines % (2 * columns) == 0
        and depth % (2 * rows) == 0
        and M % (2 * rows * columns) == 0
        and (M // rows) % 8 == 0
        and rows * (lines // columns) <= LANES
    )
    return kernel_shards(velocity) if whole_tiles else plain_shards(velocity)


def solution(mesh):
    placed = P(None, "py", "pz", None)
    return jax.shard_map(
        shards, mesh=mesh, in_specs=(placed,), out_specs=(placed, placed), check_vma=False
    )
```

time: 224 us -> 185 us (0.83)
  Pallas kernels: 220 us -> 181 us
    pallas_call x1, Pallas kernels: 220 us -> 181 us  [kernel_shards(): pl.pallas_call(functools.partial(kernel, rows, columns), out_shape=(jax.S...]
where the time goes in v3:
time: 185 us
  Pallas kernels  181 us (98%)
  local copies, waits for them, and re-layouts  3.33 us (2%)
    pallas_call x1, Pallas kernels, kernel_shards(): pl.pallas_call(functools.partial(kernel, rows, columns), out_shape=(jax.S...  181 us

profile of v3, /device:TPU:0, one launch (start us, length us, event | category | flops | bytes accessed | tf_op | source)
XLA Modules:
  0.0 185.0 jit_solution(9610668458962222448)
XLA Ops:
  0.6 181.0 %shard_map.77 = (f32[3,16,32,128]{3,2,1,0:T(8,128)}, f32[6,16,32,128]{3,2,1,0:T(8,128)}) custom-call(f32[3,40,80,320]{3,2,1,0:T(8,128)} %velocity.1, bf16[8,320,256]{2,1,0:T(8,128)(2,1)} %constant.10.clone.third_table, bf16[2,2,256,160]{3,2,1,0:T(8,128)(2,1)} %constant.11.clone.first_table, bf16[256,320]{1,0:T(8,128)(2,1)} %constant.12.clone.base_table, ...), custom_call_target="tpu_custom_call" | custom-call | tf_op jit(solution)/shard_map/pallas_call | solution.py:550
  181.7 0.0 copy-start
  181.7 2.2 %copy.10 = f32[3,16,32,128]{3,2,1,0:T(8,128)} copy(f32[3,16,32,128]{3,2,1,0:T(8,128)} %get-tuple-element.4) | data formatting | bytes 1572864
  183.9 0.0 copy-done
  183.9 1.1 copy.11
Async XLA Ops:
  181.7 2.2 %copy-start = (f32[6,16,32,128]{3,2,1,0:T(8,128)S(1)}, f32[6,16,32,128]{3,2,1,0:T(8,128)}, u32[]{:S(2)}) copy-start(f32[6,16,32,128]{3,2,1,0:T(8,128)} %get-tuple-element.5) | copy-start | bytes 4718596

commit v4 on v3

--- a/solution.py
+++ b/solution.py
@@ -76,11 +76,11 @@
 
 def kernel(
     rows, columns, velocity, third_table, first_table, base_table, direct_third_table,
-    direct_first_table, filtered, stress,
-    third, first, base, second, direct_third, direct_first, fine, lines,
+    direct_first_table, filtered_out, stress_out,
+    filtered, stress, third, first, base, second, direct_third, direct_first, fine, lines,
     send_a, recv_a, send_p, recv_p, send_b, recv_b, send_c, recv_c,
     natural, direct_lines, send_z, recv_z, send_y, recv_y, turned,
-    table_sem, load_sem, natural_sem, send_a_sem, recv_a_sem, send_p_sem, recv_p_sem,
+    out_sem, table_sem, load_sem, natural_sem, send_a_sem, recv_a_sem, send_p_sem, recv_p_sem,
     send_b_sem, recv_b_sem, send_c_sem, recv_c_sem,
     send_z_sem, recv_z_sem, send_y_sem, recv_y_sem,
 ):
@@ -104,36 +104,34 @@
         pltpu.make_async_copy(direct_first_table, direct_first, table_sem.at[3]),
     ] + [
         pltpu.make_async_copy(
-            first_table.at[mode, me_y // strides[mode] % 2], first.at[mode], table_sem.at[4 + mode]
+            first_table.at[mode, me_y // strides[mode] % 2], first.at[mode], table_sem.at[4]
         )
         for mode in range(2)
     ]
     last_left, last_right = factor_pairs[-1]
+
+    def settle(ref, sem):
+        pltpu.make_async_copy(ref, ref, sem).wait()
 
     def load_natural(u):
         return pltpu.make_async_copy(
             velocity.at[last_left, pl.ds(u * 2 * columns, 2 * columns)],
             natural.at[u % 2],
-            natural_sem.at[u],
+            natural_sem.at[u % 2],
         )
 
     def load(c):
-        def line(b, carry):
-            pltpu.make_async_copy(
-                velocity.at[c, :, b, :], fine.at[c, b % rows, b // rows], load_sem.at[c]
-            ).start()
+        def lines_of(r, carry):
+            for q in range(blocks):
+                pltpu.make_async_copy(
+                    velocity.at[c, :, q * rows + r, :], fine.at[c, r, q], load_sem.at[r]
+                ).start()
             return carry
 
-        lax.fori_loop(0, depth, line, 0)
-
-    table_copies[0].start()
-    load(0)
-    for copy in table_copies[1:]:
-        copy.start()
-    for u in range(2):
-        load_natural(u).start()
-    load(1)
-    load(2)
+        lax.fori_loop(0, rows, lines_of, 0)
+
+    def loaded(c, r):
+        settle(fine.at[c, r], load_sem.at[r])
 
     barrier = pltpu.get_barrier_semaphore()
     for k in range(1, columns):
@@ -142,7 +140,9 @@
         )
     for j in range(1, rows):
         pl.semaphore_signal(barrier, inc=1, device_id=(flip(me_y, j), me_z), device_id_type=MESH)
-    pl.semaphore_wait(barrier, columns + rows - 2)
+
+    table_copies[0].start()
+    load(0)
 
     def own_lines(mode):
         step = strides[mode]
@@ -155,8 +155,8 @@
             pltpu.make_async_remote_copy(
                 src_ref=send_a.at[f % slots_a, mode, side, u - 1],
                 dst_ref=recv_a.at[f, mode, side, :, own_lines(mode)],
-                send_sem=send_a_sem.at[f, mode, side, u - 1],
-                recv_sem=recv_a_sem.at[f, mode, side, u - 1],
+                send_sem=send_a_sem.at[f % slots_a],
+                recv_sem=recv_a_sem.at[f, mode, side],
                 device_id=(flip(me_y, j - side * step), me_z),
                 device_id_type=MESH,
             )
@@ -168,7 +168,7 @@
         return pltpu.make_async_remote_copy(
             src_ref=send_p.at[f % slots_p, mode],
             dst_ref=recv_p.at[f, mode],
-            send_sem=send_p_sem.at[f, mode],
+            send_sem=send_p_sem.at[f % slots_p, mode],
             recv_sem=recv_p_sem.at[f, mode],
             device_id=(flip(me_y, strides[mode]), me_z),
             device_id_type=MESH,
@@ -182,18 +182,25 @@
                 f % slots_b, pl.ds((me_z + k) % columns * share, share), pl.ds(mode * count, count)
             ],
             dst_ref=recv_b.at[f, :, pl.ds(pl.multiple_of(at, 8), count)],
-            send_sem=send_b_sem.at[f, mode, k - 1],
-            recv_sem=recv_b_sem.at[f, mode, k - 1],
+            send_sem=send_b_sem.at[f % slots_b, mode],
+            recv_sem=recv_b_sem.at[f],
             device_id=(me_y, (me_z + k) % columns),
             device_id_type=MESH,
         )
+
+    def free_b(f, mode):
+        count = part * rows
+        sent = send_b.at[
+            f % slots_b, pl.ds(0, (columns - 1) * share), pl.ds(mode * count, count)
+        ]
+        settle(sent, send_b_sem.at[f % slots_b, mode])
 
     def copy_c(f, j):
         return pltpu.make_async_remote_copy(
             src_ref=send_c.at[f, pl.ds(flip(me_y, j), 1)],
             dst_ref=recv_c.at[f, pl.ds(me_y, 1)],
-            send_sem=send_c_sem.at[f, j - 1],
-            recv_sem=recv_c_sem.at[f, j - 1],
+            send_sem=send_c_sem.at[0],
+            recv_sem=recv_c_sem.at[f],
             device_id=(flip(me_y, j), me_z),
             device_id_type=MESH,
         )
@@ -202,8 +209,8 @@
         return pltpu.make_async_remote_copy(
             src_ref=send_z.at[k - 1, pl.ds(2 * u, 2)],
             dst_ref=recv_z.at[pl.ds(2 * u, 2), pl.ds(pl.multiple_of(me_z * depth, 8), depth)],
-            send_sem=send_z_sem.at[u, k - 1],
-            recv_sem=recv_z_sem.at[u, k - 1],
+            send_sem=send_z_sem.at[0],
+            recv_sem=recv_z_sem.at[u],
             device_id=(me_y, (me_z + k) % columns),
             device_id_type=MESH,
         )
@@ -212,8 +219,8 @@
         return pltpu.make_async_remote_copy(
             src_ref=send_y.at[flip(me_y, j)],
             dst_ref=recv_y.at[pl.ds(me_y * steps, steps)],
-            send_sem=send_y_sem.at[j - 1],
-            recv_sem=recv_y_sem.at[j - 1],
+            send_sem=send_y_sem.at[0],
+            recv_sem=recv_y_sem.at[0],
             device_id=(flip(me_y, j), me_z),
             device_id_type=MESH,
         )
@@ -228,20 +235,23 @@
         right = jnp.where(product, right, f)
         group = lax.broadcasted_iota(jnp.int32, (near, LANES), 1) % rows
         masks = [group == flip(me_y, r) for r in range(rows)]
+
+        def piece(r, carry):
+            @pl.when(f < 3)
+            def _():
+                loaded(f, r)
+
+            value = fine[left, r] * jnp.where(product, fine[right, r], 1.0)
+            value = value.reshape(blocks * near, fine_points)
+            lines[r] = rows_times(value, third[r]).reshape(blocks, near, LANES)
+            return carry
+
+        lax.fori_loop(0, rows, piece, 0)
         for mode in range(2):
             _, tiles = spread(rows, mode)
-            where = pl.ds(mode * part, part)
-
-            def piece(r, carry):
-                value = fine[left, r, where] * jnp.where(product, fine[right, r, where], 1.0)
-                value = value.reshape(part * near, fine_points)
-                lines[r] = rows_times(value, third[r]).reshape(part, near, LANES)
-                return carry
-
-            lax.fori_loop(0, rows, piece, 0)
 
             def regroup(q, carry):
-                parts = [lines[r, q] for r in range(rows)]
+                parts = [lines[r, mode * part + q] for r in range(rows)]
                 for j, side, u in tiles:
                     out = parts[-1]
                     for r in range(rows - 1):
@@ -253,15 +263,22 @@
                 return carry
 
             lax.fori_loop(0, part, regroup, 0)
+            if mode == 0:
+
+                @pl.when(f == 0)
+                def _():
+                    pl.semaphore_wait(barrier, columns + rows - 2)
+
             for side in (1, 0):
                 for copy in copies_a(f, mode, side):
                     copy.start()
 
     def free_a(f):
-        for mode in range(2):
-            for side in (1, 0):
-                for copy in copies_a(f, mode, side):
-                    copy.wait_send()
+        settle(send_a.at[f % slots_a], send_a_sem.at[f % slots_a])
+
+    def arrived_a(f, mode, side):
+        others = (rows // 2 - 1) * near
+        settle(recv_a.at[f, mode, side, :, pl.ds(0, others)], recv_a_sem.at[f, mode, side])
 
     def table_times(table, value):
         top, rest = split(value)
@@ -278,8 +295,7 @@
 
     def first_out(f):
         for mode in range(2):
-            for copy in copies_a(f, mode, 1):
-                copy.wait_recv()
+            arrived_a(f, mode, 1)
 
             @pl.when(f >= slots_p)
             def _():
@@ -292,14 +308,12 @@
     def first_in(f):
         slot = f % slots_b
         for mode in range(2):
-            for copy in copies_a(f, mode, 0):
-                copy.wait_recv()
+            arrived_a(f, mode, 0)
             copy_p(f, mode).wait_recv()
 
             @pl.when(f >= slots_b)
             def _():
-                for k in range(1, columns):
-                    copy_b(f - slots_b, mode, k).wait_send()
+                free_b(f - slots_b, mode)
 
             count = part * rows
             for q, out in partial_first(f, mode, 0):
@@ -315,9 +329,7 @@
             ]
 
     def contract_second(f):
-        for mode in range(2):
-            for k in range(1, columns):
-                copy_b(f, mode, k).wait_recv()
+        settle(recv_b.at[f, :, pl.ds(0, (columns - 1) * depth)], recv_b_sem.at[f])
         for h in range(share // 2):
             value = jnp.concatenate([recv_b[f, 2 * h + i] for i in range(2)], axis=1)
             out = table_times(second[...], value)
@@ -329,9 +341,12 @@
             copy_c(f, j).start()
         recv_c[f, me_y] = send_c[f, me_y]
 
+    def store(f, product):
+        source, target, at = (stress, stress_out, f - 3) if product else (filtered, filtered_out, f)
+        return pltpu.make_async_copy(source.at[at], target.at[at], out_sem.at[int(product)])
+
     def place(f, product):
-        for j in range(1, rows):
-            copy_c(f, j).wait_recv()
+        settle(recv_c.at[f, pl.ds(0, rows - 1)], recv_c_sem.at[f])
         whole = recv_c.at[f].reshape(rows * share * band, M)
 
         def line(m, carry):
@@ -344,6 +359,7 @@
             return carry
 
         lax.fori_loop(0, band, line, 0)
+        store(f, product).start()
 
     def direct_contract_third():
         group = lax.broadcasted_iota(jnp.int32, (depth, LANES), 1) // block
@@ -385,8 +401,8 @@
 
     def direct_contract_second():
         def piece(h, carry):
-            for k in range(1, columns):
-                copy_z(h, k).wait_recv()
+            others = pl.ds(0, (columns - 1) * depth)
+            settle(recv_z.at[pl.ds(2 * h, 2), others], recv_z_sem.at[h])
             value = jnp.concatenate([recv_z[2 * h + i] for i in range(2)], axis=1)
             out = table_times(base[...], value)
             for i in range(2):
@@ -402,8 +418,7 @@
         recv_y[pl.ds(me_y * steps, steps)] = send_y[me_y]
 
     def direct_contract_first():
-        for j in range(1, rows):
-            copy_y(j).wait_recv()
+        settle(recv_y.at[pl.ds(0, (rows - 1) * steps)], recv_y_sem.at[0])
         pad = jnp.zeros((LANES - rows * steps, LANES), jnp.float32)
         for m in range(band):
             plane = jnp.concatenate([recv_y[:, m, :], pad], axis=0).T
@@ -415,6 +430,7 @@
             out = out + rows_times(turned[g], table)
         out = out.reshape(band, block, M)
         stress[spun - 3] = out - filtered[last_left] * filtered[last_right]
+        store(spun, True).start()
 
     def loop(start, stop, *work):
         def body(f, carry):
@@ -424,18 +440,24 @@
 
         lax.fori_loop(start, stop, body, 0)
 
-    def loaded(c):
-        pltpu.make_async_copy(fine.at[c], fine.at[c], load_sem.at[c]).wait()
-
     table_copies[0].wait()
-    loaded(0)
-    contract_third(0)
-    for copy in table_copies[1:]:
+
+    def opening(f):
+        contract_third(f)
+        load(f + 1)
+
+        @pl.when(f == 0)
+        def _():
+            for copy in table_copies[1:]:
+                copy.start()
+            for u in range(2):
+                load_natural(u).start()
+
+    loop(0, slots_a, opening)
+    for copy in table_copies[1:4]:
         copy.wait()
+    settle(first, table_sem.at[4])
     direct_contract_third()
-    loaded(1)
-    contract_third(1)
-    loaded(2)
 
     points = base.shape[1]
     row = lax.broadcasted_iota(jnp.int32, (points, points), 0)
@@ -479,24 +501,15 @@
 
     def drain_b(f):
         for mode in range(2):
-            for k in range(1, columns):
-                copy_b(f, mode, k).wait_send()
+            free_b(f, mode)
 
     loop(spun - slots_b, spun, drain_b)
 
-    def drain_c(f):
-        for j in range(1, rows):
-            copy_c(f, j).wait_send()
-
-    loop(0, spun, drain_c)
-
-    def drain_z(u):
-        for k in range(1, columns):
-            copy_z(u, k).wait_send()
-
-    loop(0, steps // 2, drain_z)
-    for j in range(1, rows):
-        copy_y(j).wait_send()
+    settle(send_c.at[:, pl.ds(0, rows - 1)], send_c_sem.at[0])
+    settle(send_z, send_z_sem.at[0])
+    settle(send_y.at[pl.ds(0, rows - 1)], send_y_sem.at[0])
+    settle(filtered, out_sem.at[0])
+    settle(stress, out_sem.at[1])
 
 
 def tables(fine, rows, columns):
@@ -544,7 +557,6 @@
     slots_a, slots_p, slots_b = 2, 2, 2
     constants = tables(fine, rows, columns)
     third, first, base, direct_third, direct_first = constants
-    vmem = pl.BlockSpec(memory_space=pltpu.VMEM)
     dma = pltpu.SemaphoreType.DMA
     f32, bf16 = jnp.float32, jnp.bfloat16
     return pl.pallas_call(
@@ -554,8 +566,10 @@
             jax.ShapeDtypeStruct((6, band, block, M), f32),
         ),
         in_specs=[pl.BlockSpec(memory_space=pl.ANY)] * (1 + len(constants)),
-        out_specs=(vmem, vmem),
+        out_specs=(pl.BlockSpec(memory_space=pl.ANY),) * 2,
         scratch_shapes=[
+            pltpu.VMEM((3, band, block, M), f32),
+            pltpu.VMEM((6, band, block, M), f32),
             pltpu.VMEM(third.shape, bf16),
             pltpu.VMEM(first.shape[1:], bf16),
             pltpu.VMEM(base.shape, bf16),
@@ -563,7 +577,7 @@
             pltpu.VMEM(direct_third.shape, bf16),
             pltpu.VMEM(direct_first.shape, bf16),
             pltpu.VMEM((3, rows, blocks, near, fine), f32),
-            pltpu.VMEM((rows, part, near, LANES), f32),
+            pltpu.VMEM((rows, blocks, near, LANES), f32),
             pltpu.VMEM((slots_a, 2, 2, half - 1, part, near, LANES), f32),
             pltpu.VMEM((spun, 2, 2, part, half * near, LANES), f32),
             pltpu.VMEM((slots_p, 2, part, M, LANES), f32),
@@ -579,21 +593,22 @@
             pltpu.VMEM((rows, steps, band, LANES), f32),
             pltpu.VMEM((rows * steps, band, LANES), f32),
             pltpu.VMEM((columns, band * block, LANES), f32),
-            dma((6,)),
-            dma((3,)),
+            dma((2,)),
+            dma((5,)),
+            dma((rows,)),
+            dma((2,)),
+            dma((slots_a,)),
+            dma((spun, 2, 2)),
+            dma((slots_p, 2)),
+            dma((spun, 2)),
+            dma((slots_b, 2)),
+            dma((spun,)),
+            dma((1,)),
+            dma((spun,)),
+            dma((1,)),
             dma((steps // 2,)),
-            dma((spun, 2, 2, half - 1)),
-            dma((spun, 2, 2, half - 1)),
-            dma((spun, 2)),
-            dma((spun, 2)),
-            dma((spun, 2, columns - 1)),
-            dma((spun, 2, columns - 1)),
-            dma((spun, rows - 1)),
-            dma((spun, rows - 1)),
-            dma((steps // 2, columns - 1)),
-            dma((steps // 2, columns - 1)),
-            dma((rows - 1,)),
-            dma((rows - 1,)),
+            dma((1,)),
+            dma((1,)),
         ],
         compiler_params=pltpu.CompilerParams(
             collective_id=0, has_side_effects=True, vmem_limit_bytes=67_000_000

time: 185 us -> 175 us (0.946)
  Pallas kernels: 181 us -> 170 us
    pallas_call x1, Pallas kernels: 181 us -> 170 us  [kernel_shards(): pl.pallas_call(functools.partial(kernel, rows, columns), out_shape=(jax.S...]
where the time goes in v4:
time: 175 us; the launch traced here: 174 us
  Pallas kernels  170 us (97%)
  local copies, waits for them, and re-layouts  3.33 us (2%)
    pallas_call x1, Pallas kernels, kernel_shards(): pl.pallas_call(functools.partial(kernel, rows, columns), out_shape=(jax.S...  170 us

profile of v4, /device:TPU:0, one launch (start us, length us, event | category | flops | bytes accessed | tf_op | source)
XLA Modules:
  0.0 174.3 jit_solution(13617469683491574763)
XLA Ops:
  0.6 170.3 %shard_map.77 = (f32[3,16,32,128]{3,2,1,0:T(8,128)}, f32[6,16,32,128]{3,2,1,0:T(8,128)}) custom-call(f32[3,40,80,320]{3,2,1,0:T(8,128)} %velocity.1, bf16[8,320,256]{2,1,0:T(8,128)(2,1)} %constant.10.clone.third_table, bf16[2,2,256,160]{3,2,1,0:T(8,128)(2,1)} %constant.11.clone.first_table, bf16[256,320]{1,0:T(8,128)(2,1)} %constant.12.clone.base_table, ...), custom_call_target="tpu_custom_call" | custom-call | tf_op jit(solution)/shard_map/pallas_call | solution.py:562
  170.9 0.0 copy-start
  170.9 2.2 %copy.10 = f32[3,16,32,128]{3,2,1,0:T(8,128)} copy(f32[3,16,32,128]{3,2,1,0:T(8,128)} %get-tuple-element.4) | data formatting | bytes 1572864
  173.1 0.0 copy-done
  173.1 1.1 copy.11
Async XLA Ops:
  170.9 2.2 %copy-start = (f32[6,16,32,128]{3,2,1,0:T(8,128)S(1)}, f32[6,16,32,128]{3,2,1,0:T(8,128)}, u32[]{:S(2)}) copy-start(f32[6,16,32,128]{3,2,1,0:T(8,128)} %get-tuple-element.5) | copy-start | bytes 4718596

commit v5 on v4

--- a/solution.py
+++ b/solution.py
@@ -143,6 +143,10 @@
 
     table_copies[0].start()
     load(0)
+    for u in range(2):
+        load_natural(u).start()
+    for copy in table_copies[1:]:
+        copy.start()
 
     def own_lines(mode):
         step = strides[mode]
@@ -361,7 +365,7 @@
         lax.fori_loop(0, band, line, 0)
         store(f, product).start()
 
-    def direct_contract_third():
+    def direct_contract_third(begin, end):
         group = lax.broadcasted_iota(jnp.int32, (depth, LANES), 1) // block
         masks = [group == (me_z + k) % columns for k in range(columns)]
         units = steps // 2
@@ -397,7 +401,7 @@
                 copy_z(u, k).start()
             return carry
 
-        lax.fori_loop(0, units, unit, 0)
+        lax.fori_loop(begin, end, unit, 0)
 
     def direct_contract_second():
         def piece(h, carry):
@@ -444,20 +448,17 @@
 
     def opening(f):
         contract_third(f)
-        load(f + 1)
 
         @pl.when(f == 0)
         def _():
-            for copy in table_copies[1:]:
-                copy.start()
-            for u in range(2):
-                load_natural(u).start()
+            for copy in table_copies[1:4]:
+                copy.wait()
+            settle(first, table_sem.at[4])
+
+        load(f + 1)
+        direct_contract_third(f, 1 + f * (steps // 2 - 1))
 
     loop(0, slots_a, opening)
-    for copy in table_copies[1:4]:
-        copy.wait()
-    settle(first, table_sem.at[4])
-    direct_contract_third()
 
     points = base.shape[1]
     row = lax.broadcasted_iota(jnp.int32, (points, points), 0)

time: 175 us -> 171 us (0.977)
  Pallas kernels: 170 us -> 167 us
    pallas_call x1, Pallas kernels: 170 us -> 167 us  [kernel_shards(): pl.pallas_call(functools.partial(kernel, rows, columns), out_shape=(jax.S...]
where the time goes in v5:
time: 171 us
  Pallas kernels  167 us (98%)
  local copies, waits for them, and re-layouts  3.33 us (2%)
    pallas_call x1, Pallas kernels, kernel_shards(): pl.pallas_call(functools.partial(kernel, rows, columns), out_shape=(jax.S...  167 us

profile of v5, /device:TPU:0, one launch (start us, length us, event | category | flops | bytes accessed | tf_op | source)
XLA Modules:
  0.0 171.1 jit_solution(362433808166742216)
XLA Ops:
  0.6 167.1 %shard_map.77 = (f32[3,16,32,128]{3,2,1,0:T(8,128)}, f32[6,16,32,128]{3,2,1,0:T(8,128)}) custom-call(f32[3,40,80,320]{3,2,1,0:T(8,128)} %velocity.1, bf16[8,320,256]{2,1,0:T(8,128)(2,1)} %constant.10.clone.third_table, bf16[2,2,256,160]{3,2,1,0:T(8,128)(2,1)} %constant.11.clone.first_table, bf16[256,320]{1,0:T(8,128)(2,1)} %constant.12.clone.base_table, ...), custom_call_target="tpu_custom_call" | custom-call | tf_op jit(solution)/shard_map/pallas_call | solution.py:563
  167.7 0.0 copy-start
  167.7 2.2 %copy.10 = f32[3,16,32,128]{3,2,1,0:T(8,128)} copy(f32[3,16,32,128]{3,2,1,0:T(8,128)} %get-tuple-element.4) | data formatting | bytes 1572864
  169.9 0.0 copy-done
  169.9 1.1 copy.11
Async XLA Ops:
  167.7 2.2 %copy-start = (f32[6,16,32,128]{3,2,1,0:T(8,128)S(1)}, f32[6,16,32,128]{3,2,1,0:T(8,128)}, u32[]{:S(2)}) copy-start(f32[6,16,32,128]{3,2,1,0:T(8,128)} %get-tuple-element.5) | copy-start | bytes 4718596

commit v6 on v5

--- a/solution.py
+++ b/solution.py
@@ -469,14 +469,14 @@
     def round_of(f):
         first_out(f)
 
+        @pl.when(f >= 1)
+        def _():
+            first_in(f - 1)
+
         @pl.when(f + slots_a < spun)
         def _():
             free_a(f)
             contract_third(f + slots_a)
-
-        @pl.when(f >= 1)
-        def _():
-            first_in(f - 1)
 
     loop(0, spun - 1, round_of)
     first_out(spun - 1)

time: 171 us -> 171 us (level)
  no operation moved by 1% of the time
where the time goes in v6:
time: 171 us
  Pallas kernels  167 us (98%)
  local copies, waits for them, and re-layouts  3.33 us (2%)
    pallas_call x1, Pallas kernels, kernel_shards(): pl.pallas_call(functools.partial(kernel, rows, columns), out_shape=(jax.S...  167 us

profile of v6, /device:TPU:0, one launch (start us, length us, event | category | flops | bytes accessed | tf_op | source)
XLA Modules:
  0.0 171.1 jit_solution(3480691533744851560)
XLA Ops:
  0.6 167.1 %shard_map.77 = (f32[3,16,32,128]{3,2,1,0:T(8,128)}, f32[6,16,32,128]{3,2,1,0:T(8,128)}) custom-call(f32[3,40,80,320]{3,2,1,0:T(8,128)} %velocity.1, bf16[8,320,256]{2,1,0:T(8,128)(2,1)} %constant.10.clone.third_table, bf16[2,2,256,160]{3,2,1,0:T(8,128)(2,1)} %constant.11.clone.first_table, bf16[256,320]{1,0:T(8,128)(2,1)} %constant.12.clone.base_table, ...), custom_call_target="tpu_custom_call" | custom-call | tf_op jit(solution)/shard_map/pallas_call | solution.py:563
  167.7 0.0 copy-start
  167.7 2.2 %copy.10 = f32[3,16,32,128]{3,2,1,0:T(8,128)} copy(f32[3,16,32,128]{3,2,1,0:T(8,128)} %get-tuple-element.4) | data formatting | bytes 1572864
  169.9 0.0 copy-done
  169.9 1.1 copy.11
Async XLA Ops:
  167.7 2.2 %copy-start = (f32[6,16,32,128]{3,2,1,0:T(8,128)S(1)}, f32[6,16,32,128]{3,2,1,0:T(8,128)}, u32[]{:S(2)}) copy-start(f32[6,16,32,128]{3,2,1,0:T(8,128)} %get-tuple-element.5) | copy-start | bytes 4718596
